TPU v7x, 32 devices: a whole 2x2x4 slice. The times are simulated.
32 devices in a mesh: row: 4 (over x, core), col: 8 (over z, y).
Axes of the slice: x: 2, y: 2, z: 4, core: 2. Of those that a mesh axis runs over, the one named last changes fastest.
Arguments:
- normed: bfloat16 [12288, 6144], P(('row', 'col')), may hold values from -6 to 6
- out_grad: bfloat16 [12288, 6144], P(('row', 'col')), may hold values from -0.125 to 0.125
- w_in: bfloat16 [6144, 48], replicated, may hold values from -0.078125 to 0.078125
- hidden_grad: bfloat16 [12288, 48], P(('row', 'col')), may hold values from -0.125 to 0.125
- qkv_grad: bfloat16 [12288, 64], P(('row', 'col')), may hold values from -0.125 to 0.125
- bucket_order: int32 [160], replicated, may hold values from 0 to 159, each once
Outputs:
- buckets: bfloat16 [160, 6144], replicated
Inputs may be any that keep to these rules, and one draw needn't show every extreme that they name: bucket_order is a permutation of 0 to 159.
All inputs are finite; a program needn't handle non-finite values.
Results may differ from a plain program's by a relative error of at most 0.0044.
Values may be sent and summed in bfloat16 or wider, within the bound.
A program may use at most 64 MiB of HBM per device.

v0:
```python
import jax
import jax.numpy as jnp
from jax import lax
from jax.sharding import PartitionSpec as P

NB = 4


def local(normed, out_grad, w_in, hidden_grad, qkv_grad, bucket_order):
    pre = jnp.dot(normed, w_in, preferred_element_type=jnp.float32)
    cdf = 0.5 * (1.0 + lax.erf(pre * 0.7071067811865476))
    pdf = jnp.exp(-0.5 * pre * pre) * 0.3989422804014327
    hidden = (pre * cdf).astype(jnp.bfloat16)
    pre_grad = (hidden_grad.astype(jnp.float32) * (cdf + pre * pdf)).astype(jnp.bfloat16)
    grad_qkv = jnp.dot(qkv_grad.T, normed, preferred_element_type=jnp.float32)
    grad_in = jnp.dot(pre_grad.T, normed, preferred_element_type=jnp.float32)
    grad_out = jnp.dot(hidden.T, out_grad, preferred_element_type=jnp.float32)
    stacked = jnp.concatenate([grad_qkv, grad_in, grad_out], axis=0)
    ordered = jnp.take(stacked, bucket_order, axis=0)
    per_bucket = ordered.shape[0] // NB
    results = []
    for bucket in range(NB):
        piece = ordered[bucket * per_bucket : (bucket + 1) * per_bucket]
        summed = lax.psum(piece, ("row", "col")).astype(jnp.bfloat16)
        results.append(summed)
    return jnp.concatenate(results, axis=0)


def solution(mesh):
    in_specs = (
        P(("row", "col"), None),
        P(("row", "col"), None),
        P(),
        P(("row", "col"), None),
        P(("row", "col"), None),
        P(),
    )
    out_specs = P()
    return jax.shard_map(local, mesh=mesh, in_specs=in_specs, out_specs=out_specs, check_vma=False)
```

profile of v0, /device:TPU:0, one launch (start us, length us, event | category | flops | bytes accessed | tf_op | source)
XLA Modules:
  0.0 118.2 jit_solution(10145399101433720630)
XLA Ops:
  0.0 0.0 copy-start
  0.0 0.0 copy-start.2
  0.0 1.1 copy-done
  1.1 4.3 %fusion.15 = f32[384,48]{0,1:T(8,128)S(1)} fusion(bf16[384,6144]{1,0:T(8,128)(2,1)} %param.6, bf16[6144,48]{0,1:T(8,128)(2,1)S(1)} %copy-done), kind=kOutput, calls=%fused_computation.24 | convolution fusion | flops 226492416 | bytes 5382144 | tf_op jit(solution)/shard_map/dot_general | solution.py:10
  5.4 0.0 copy-done.2
  5.4 0.0 copy-start.1
  5.4 0.0 copy-start.4
  5.4 0.9 fusion.6
  6.4 1.4 %copy-done.1 = bf16[384,6144]{1,0:T(8,128)(2,1)S(1)} copy-done((bf16[384,6144]{1,0:T(8,128)(2,1)S(1)}, bf16[384,6144]{1,0:T(8,128)(2,1)}, u32[]{:S(2)}) %copy-start.1) | copy-done | bytes 4718616
  7.7 0.0 copy-done.4
  7.7 0.0 copy-start.3
  7.7 0.9 fusion.7
  8.7 0.0 copy-done.3
  8.7 0.9 fusion.14
  9.6 0.0 copy-start.5
  9.7 2.1 %pad_maximum_fusion = f32[160,6144]{1,0:T(8,128)} fusion(f32[48,6144]{1,0:T(8,128)S(1)} %fusion.6, f32[48,6144]{1,0:T(8,128)S(1)} %fusion.7, f32[64,6144]{1,0:T(8,128)S(1)} %fusion.14), kind=kLoop, calls=%fused_computation.1 | loop fusion | flops 1966080 | bytes 7864320 | tf_op jit(solution)/shard_map/concatenate | solution.py:18
  11.8 0.0 copy-done.5
  11.8 7.4 %gather_fusion = f32[160,6144]{1,0:T(8,128)} fusion(f32[160,6144]{1,0:T(8,128)} %pad_maximum_fusion, s32[1024]{0:T(1024)S(1)} %pad_clamp_fusion), kind=kCustom, calls=%fused_computation | custom fusion | bytes 7864960 | tf_op jit(solution)/shard_map/jit(_take)/gather | solution.py:19
  19.3 2.7 %broadcast_select_fusion = f32[160,6144]{1,0:T(8,128)S(1)} fusion(f32[160,6144]{1,0:T(8,128)} %gather_fusion, pred[160]{0:T(512)(128)(4,1)S(1)} %compare_and_fusion), kind=kLoop, calls=%fused_computation.3 | loop fusion | flops 983040 | bytes 7864480 | tf_op jit(solution)/shard_map/jit(_take)/select_n | solution.py:19
  22.0 1.2 %fusion.13 = (f32[40,6144]{1,0:T(8,128)S(1)}, f32[40,6144]{1,0:T(8,128)S(1)}, f32[40,6144]{1,0:T(8,128)S(1)}, f32[40,6144]{1,0:T(8,128)}) fusion(f32[160,6144]{1,0:T(8,128)S(1)} %broadcast_select_fusion), kind=kLoop, calls=%fused_computation.22 | loop fusion | bytes 7864320 | tf_op jit(solution)/shard_map/slice | solution.py:23
  23.2 92.1 %all-reduce.2 = (bf16[40,6144]{1,0:T(8,128)(2,1)}, bf16[40,6144]{1,0:T(8,128)(2,1)}, bf16[40,6144]{1,0:T(8,128)(2,1)}, bf16[40,6144]{1,0:T(8,128)(2,1)}) all-reduce(f32[40,6144]{1,0:T(8,128)S(1)} %get-tuple-element.10, f32[40,6144]{1,0:T(8,128)S(1)} %get-tuple-element.11, ...), channel_id=1, replica_groups=mesh['row'=4,'col'=8] {'row','col'}, use_global_device_ids=true, to_apply=%region_3.4 | all-reduce | flops 983040 | bytes 5898240 | tf_op jit(solution)/shard_map/psum | solution.py:24
  115.3 2.9 %pad_maximum_fusion.1 = bf16[160,6144]{1,0:T(8,128)(2,1)} fusion(bf16[40,6144]{1,0:T(8,128)(2,1)} %get-tuple-element.5, bf16[40,6144]{1,0:T(8,128)(2,1)} %get-tuple-element.6, bf16[40,6144]{1,0:T(8,128)(2,1)} %get-tuple-element.7, bf16[40,6144]{1,0:T(8,128)(2,1)} %get-tuple-element.8), kind=kLoop, calls=%fused_computation.2 | loop fusion | flops 7864320 | bytes 3932160 | tf_op jit(solution)/shard_map/concatenate | solution.py:26
  (3 shorter events, 0.0 us)
Async XLA Ops:
  0.0 1.1 copy-start
  0.0 5.4 %copy-start.2 = (bf16[384,6144]{1,0:T(8,128)(2,1)S(1)}, bf16[384,6144]{1,0:T(8,128)(2,1)}, u32[]{:S(2)}) copy-start(bf16[384,6144]{1,0:T(8,128)(2,1)} %param.7) | copy-start | bytes 14155780
  5.4 2.3 %copy-start.1 = (bf16[384,6144]{1,0:T(8,128)(2,1)S(1)}, bf16[384,6144]{1,0:T(8,128)(2,1)}, u32[]{:S(2)}) copy-start(bf16[384,6144]{1,0:T(8,128)(2,1)} %param.6) | copy-start | bytes 14155780
  5.4 2.3 %copy-start.4 = (bf16[384,48]{0,1:T(8,128)(2,1)S(1)}, bf16[384,48]{0,1:T(8,128)(2,1)}, u32[]{:S(2)}) copy-start(bf16[384,48]{0,1:T(8,128)(2,1)} %param.9) | copy-start | bytes 110596
  7.7 0.9 copy-start.3
  9.6 2.2 %copy-start.5 = (s32[160]{0:T(256)S(1)}, s32[160]{0:T(256)}, u32[]{:S(2)}) copy-start(s32[160]{0:T(256)} %param.11) | copy-start | bytes 1924
where the time goes:
time: 118 us
  blocking collectives  92.1 us (78%)
  local copies, waits for them, and re-layouts  11.1 us (9%)
  other arithmetic  7.78 us (7%)
  matrix products  7.13 us (6%)
    psum x1, blocking collectives, local(): summed = lax.psum(piece, ('row', 'col')).astype(jnp.bfloat16)  92.1 us
    gather x1, local copies, waits for them, and re-layouts, local(): ordered = jnp.take(stacked, bucket_order, axis=0)  7.44 us
    dot_general x1, matrix products, local(): pre = jnp.dot(normed, w_in, preferred_element_type=jnp.float32)  4.31 us
    concatenate x1, other arithmetic, local(): return jnp.concatenate(results, axis=0)  2.92 us
    select_n x2, other arithmetic, local(): ordered = jnp.take(stacked, bucket_order, axis=0)  2.7 us
    unnamed x12, local copies, waits for them, and re-layouts  2.46 us

commit v1 on v0

--- a/solution.py
+++ b/solution.py
@@ -21,7 +21,7 @@
     results = []
     for bucket in range(NB):
         piece = ordered[bucket * per_bucket : (bucket + 1) * per_bucket]
-        summed = lax.psum(piece, ("row", "col")).astype(jnp.bfloat16)
+        summed = lax.psum(lax.psum(piece, "row"), "col").astype(jnp.bfloat16)
         results.append(summed)
     return jnp.concatenate(results, axis=0)
 

time: 118 us -> 280 us (2.37)
  waiting for transfers between devices: 0 us -> 84.2 us
  blocking collectives: 92.1 us -> 157 us
  between operations: 0.08 us -> 13.5 us
    psum x0 -> x1, waiting for transfers between devices: none -> 84.2 us  [local(): summed = lax.psum(lax.psum(piece, 'row'), 'col').astype(jnp.bfloat16)]
    psum x1, blocking collectives: 92.1 us -> 157 us  [local(): summed = lax.psum(lax.psum(piece, 'row'), 'col').astype(jnp.bfloat16)]
  transfers between devices with their start and end apart: 0 -> 1, of which waited for: 0 -> 1; matrix products, arithmetic and copies ran while one was open for 0% -> 0% of each run, Pallas kernels for 0% -> 0%
where the time goes in v1:
time: 280 us
  blocking collectives  157 us (56%)
  waiting for transfers between devices  84.2 us (30%)
  between operations  13.5 us (5%)
  local copies, waits for them, and re-layouts  10.8 us (4%)
  other arithmetic  8.19 us (3%)
  matrix products  6.64 us (2%)
    psum x1, blocking collectives, local(): summed = lax.psum(lax.psum(piece, 'row'), 'col').astype(jnp.bfloat16)  157 us
    psum x1, waiting for transfers between devices, local(): summed = lax.psum(lax.psum(piece, 'row'), 'col').astype(jnp.bfloat16)  84.2 us
    gather x1, local copies, waits for them, and re-layouts, local(): ordered = jnp.take(stacked, bucket_order, axis=0)  7.44 us
  transfers between devices with their start and end apart: 1, of which 1 were waited for; matrix products, arithmetic and copies ran while one was open for 0% of the time, Pallas kernels for 0%

profile of v1, /device:TPU:0, one launch (start us, length us, event | category | flops | bytes accessed | tf_op | source)
XLA Modules:
  0.0 280.1 jit_solution(4870922449635941462)
XLA Ops:
  6.5 0.0 copy-start
  6.5 0.0 all-reduce.5.cloned.1.call-start
  6.5 0.0 copy-start.2
  6.5 0.8 compare_select_fusion
  7.4 1.1 compare_and_fusion
  8.5 0.0 copy-done
  8.5 3.8 %fusion.15 = f32[384,48]{0,1:T(8,128)S(1)} fusion(bf16[384,6144]{1,0:T(8,128)(2,1)} %param.6, bf16[6144,48]{0,1:T(8,128)(2,1)S(1)} %copy-done), kind=kOutput, calls=%fused_computation.24 | convolution fusion | flops 226492416 | bytes 5382144 | tf_op jit(solution)/shard_map/dot_general | solution.py:10
  12.3 0.0 copy-done.2
  12.3 0.0 copy-start.1
  12.3 0.0 copy-start.4
  12.3 0.9 fusion.6
  13.3 1.4 copy-done.1
  14.6 0.0 copy-done.4
  14.6 0.0 copy-start.3
  14.6 0.9 fusion.7
  15.6 0.0 copy-done.3
  15.6 0.9 fusion.14
  16.6 2.2 pad_maximum_fusion
  18.7 7.4 %gather_fusion = f32[160,6144]{1,0:T(8,128)} fusion(f32[160,6144]{1,0:T(8,128)} %pad_maximum_fusion, s32[1024]{0:T(1024)S(1)} %pad_clamp_fusion), kind=kCustom, calls=%fused_computation | custom fusion | bytes 7864960 | tf_op jit(solution)/shard_map/jit(_take)/gather | solution.py:19
  26.2 2.7 broadcast_select_fusion
  28.9 2.0 fusion.13
  30.9 0.0 all-reduce.5.cloned.1.call-update
  30.9 84.2 %all-reduce.5.cloned.1.call-done = (f32[40,6144]{1,0:T(8,128)}, f32[40,6144]{1,0:T(8,128)}, f32[40,6144]{1,0:T(8,128)}, f32[40,6144]{1,0:T(8,128)}) async-done(((f32[40,6144]{1,0:T(8,128)}, f32[40,6144]{1,0:T(8,128)}, f32[40,6144]{1,0:T(8,128)}, f32[40,6144]{1,0:T(8,128)}), (f32[40,6144]{1,0:T(8,128)}, f32[40,6144]{1,0:T(8,128)}, f32[40,6144]{1,0:T(8,128)}, ...) | async-done | bytes 3932176 | tf_op jit(solution)/shard_map/psum | solution.py:24
  115.1 156.8 %all-reduce.6 = (bf16[40,6144]{1,0:T(8,128)(2,1)S(1)}, bf16[40,6144]{1,0:T(8,128)(2,1)S(1)}, bf16[40,6144]{1,0:T(8,128)(2,1)S(1)}, bf16[40,6144]{1,0:T(8,128)(2,1)S(1)}) all-reduce(f32[40,6144]{1,0:T(8,128)} %get-tuple-element.9, f32[40,6144]{1,0:T(8,128)} %get-tuple-element.10, ...), channel_id=1, replica_groups=mesh['row'=4,'col'=8] {'col'}, use_global_device_ids=true, to_apply=%region_7.8 | all-reduce | flops 983040 | bytes 5898240 | tf_op jit(solution)/shard_map/psum | solution.py:24
  271.9 1.4 pad_maximum_fusion.1
  (1 shorter events, 0.0 us)
Async XLA Ops:
  6.5 1.9 copy-start
  6.5 108.5 %all-reduce.5.cloned.1.call-start = ((), (), s32[]{:S(2)}) async-start(), calls=%async_computation | async-start | bytes 7864320 | tf_op jit(solution)/shard_map/psum | solution.py:24
  6.5 5.8 %copy-start.2 = (bf16[384,6144]{1,0:T(8,128)(2,1)S(1)}, bf16[384,6144]{1,0:T(8,128)(2,1)}, u32[]{:S(2)}) copy-start(bf16[384,6144]{1,0:T(8,128)(2,1)} %param.7) | copy-start | bytes 14155780
  12.3 2.3 copy-start.1
  12.3 2.3 copy-start.4
  14.6 0.9 copy-start.3
Sparse Core Ops, SparseCore 0:
  31.0 83.9 all-reduce.4
